TPU v7x, 32 devices: a whole 2x2x4 slice. The times are simulated.
32 devices in a mesh: groups: 2 (over y), dom: 4 (over z), sub: 2 (over x), field: 2 (over core).
Axes of the slice: x: 2, y: 2, z: 4, core: 2. Of those that a mesh axis runs over, the one named last changes fastest.
Arguments:
- background: float32 [3, 65536], P(None, ('groups', 'dom', 'sub')), parts along dimension 1, may hold values from -6 to 6
- obs_weight: float32 [65536], P(('groups', 'dom', 'sub')), parts along dimension 0, may hold values from 0.02 to 0.2
- connect: int32 [10, 32768], P(None, ('groups', 'dom', 'sub', 'field')), parts along dimension 1, may hold values from 0 to 5631, as said below
- live_blocks: int32 [32], P(('groups', 'dom', 'sub', 'field')), parts along dimension 0, may hold values from 2 to 8, as said below
- elem_scale: float32 [32768], P(('groups', 'dom', 'sub', 'field')), parts along dimension 0, may hold values from 0.5 to 2
- reg_weight: float32 [32768], P(('groups', 'dom', 'sub', 'field')), parts along dimension 0, may hold values from 0.2 to 2
- iterate: float32 [32768], P(('groups', 'dom', 'sub', 'field')), parts along dimension 0, may hold values from -6 to 6
- residual: float32 [32768], P(('groups', 'dom', 'sub', 'field')), parts along dimension 0, may hold values from -30 to 30
- direction: float32 [32768], P(('groups', 'dom', 'sub', 'field')), parts along dimension 0, may hold values from -30 to 30
- send_nodes: int32 [16, 3, 2, 256], P(('groups', 'dom', 'sub')), parts along dimension 0, may hold values from 0 to 4095, as said below
- send_count: int32 [16, 3, 2], P(('groups', 'dom', 'sub')), parts along dimension 0, may hold values from 0 to 256, as said below
- ref_stiff: float32 [30, 30], replicated, may hold values from -1.05 to 4.05, as said below
Outputs:
- iterate_next: float32 [32768], P(('groups', 'dom', 'sub', 'field')), parts along dimension 0
- residual_next: float32 [32768], P(('groups', 'dom', 'sub', 'field')), parts along dimension 0
- direction_next: float32 [32768], P(('groups', 'dom', 'sub', 'field')), parts along dimension 0
There are 2 independent parts, one for each index of `groups`. A program takes and returns all parts, laid end to end along the dimension named above; an argument that names none is the same for every part. Nothing has to cross between parts.
Inputs may be any that keep to these rules, and one draw needn't show every extreme that they name: `send_nodes`: for every link the first send_count slots hold distinct owned nodes; later slots are padding. `send_count`: links go only to partitions of dom index d - 1, d or d + 1 and never to the sender itself or past the ends of dom; some link is full with 256 slots. `connect`: entries from 4096 on name ghost slots that are live slots of their owner's link. `live_blocks`: live blocks fill a device's slots from its first one; some device has 8. `ref_stiff`: Symmetric.
All inputs are finite; a program needn't handle non-finite values.
Results may differ from a plain program's by a relative error of at most 0.00005.
Values sent between devices are 32-bit elements; how exact they have to be, the bound alone decides.
A program may use at most 64 MiB of HBM per device.

v0:
```python
import jax
import jax.numpy as jnp
from jax import lax
from jax.sharding import PartitionSpec as P

BLK = 128


def extended(cells, sides, width):
    for axis, dim in sides:
        count = lax.axis_size(axis)
        ends = count - 1
        head = lax.slice_in_dim(cells, 0, width, axis=dim)
        tail = lax.slice_in_dim(cells, cells.shape[dim] - width, cells.shape[dim], axis=dim)
        cells = jnp.concatenate(
            [
                lax.ppermute(tail, axis, [(i, (i + 1) % count) for i in range(ends)]),
                cells,
                lax.ppermute(head, axis, [((i + 1) % count, i) for i in range(ends)]),
            ],
            axis=dim,
        )
    return cells


def on_device(
    background,
    obs_weight,
    connect,
    live_blocks,
    elem_scale,
    reg_weight,
    iterate,
    residual,
    direction,
    send_nodes,
    send_count,
    ref_stiff,
):
    owned_nodes = background.shape[1]
    sub_count = lax.axis_size("sub")
    link_slots = send_nodes.shape[3]
    element_count = connect.shape[1]
    ghost_slots = 3 * sub_count * link_slots
    targets = send_nodes[0].reshape(-1)
    open_slot = (
        jnp.arange(link_slots, dtype=jnp.int32)[None, None, :] < send_count[0][:, :, None]
    ).astype(jnp.float32)

    def fetch_ghosts(values):
        outbound = values[:, targets].reshape(3, 3, sub_count, link_slots) * open_slot[None]
        mixed = lax.all_to_all(outbound, "sub", split_axis=2, concat_axis=2, tiled=True)
        rimmed = extended(mixed, (("dom", 1),), 1)
        arrived = rimmed[:, 0::2]
        return jnp.concatenate([values, arrived.reshape(3, ghost_slots)], axis=1)

    element = jnp.arange(element_count, dtype=jnp.int32)
    live_mask = (element < BLK * live_blocks[0]).astype(jnp.float32)
    search = live_mask * direction
    remain = live_mask * residual
    guess = live_mask * iterate
    flat_connect = connect.reshape(-1)
    state_full = fetch_ghosts(background)
    element_state = state_full[:, connect].reshape(30, element_count)
    coupled = (live_mask * elem_scale)[None, :] * jnp.dot(
        ref_stiff, element_state, precision=lax.Precision.HIGHEST
    )
    terms = (search[None, :] * coupled).reshape(3, -1)
    accumulated = (
        jnp.zeros((3, owned_nodes + ghost_slots), jnp.float32).at[:, flat_connect].add(terms)
    )
    accumulated = lax.psum(accumulated, "field")
    returning = accumulated[:, owned_nodes:].reshape(3, 3, sub_count, link_slots)
    rimmed = extended(returning, (("dom", 1),), 1)
    landed = lax.all_to_all(rimmed[:, 0::2], "sub", split_axis=2, concat_axis=2, tiled=True)
    landed = (landed * open_slot[None]).reshape(3, -1)
    assembled = accumulated[:, :owned_nodes] + jnp.zeros((3, owned_nodes), jnp.float32).at[
        :, targets
    ].add(landed)
    weighted = obs_weight[None, :] * assembled
    weighted_full = fetch_ghosts(weighted)
    pulled = weighted_full[:, connect].reshape(30, element_count)
    hess_search = jnp.sum(coupled * pulled, axis=0) + reg_weight * search
    squared_before, curvature_sum, cross_term, image_square = lax.psum(
        (
            jnp.sum(remain * remain),
            jnp.sum(search * hess_search),
            jnp.sum(remain * hess_search),
            jnp.sum(hess_search * hess_search),
        ),
        ("dom", "sub", "field"),
    )
    step_length = squared_before / curvature_sum
    iterate_next = guess + step_length * search
    residual_next = remain - step_length * hess_search
    squared_after = (
        squared_before - 2.0 * step_length * cross_term + step_length * step_length * image_square
    )
    direction_next = residual_next + squared_after / squared_before * search
    return (iterate_next, residual_next, direction_next)


def solution(mesh):
    placed = (
        P(None, ("groups", "dom", "sub")),
        P(("groups", "dom", "sub")),
        P(None, ("groups", "dom", "sub", "field")),
        P(("groups", "dom", "sub", "field")),
        P(("groups", "dom", "sub", "field")),
        P(("groups", "dom", "sub", "field")),
        P(("groups", "dom", "sub", "field")),
        P(("groups", "dom", "sub", "field")),
        P(("groups", "dom", "sub", "field")),
        P(("groups", "dom", "sub"), None, None, None),
        P(("groups", "dom", "sub"), None, None),
        P(),
    )
    return jax.shard_map(
        on_device,
        mesh=mesh,
        in_specs=placed,
        out_specs=(
            P(("groups", "dom", "sub", "field")),
            P(("groups", "dom", "sub", "field")),
            P(("groups", "dom", "sub", "field")),
        ),
        check_vma=False,
    )
```

profile of v0, /device:TPU:0, one launch (start us, length us, event | category | flops | bytes accessed | tf_op | source)
XLA Modules:
  0.0 283.6 jit_solution(14023031561616133790)
XLA Ops:
  7.2 0.0 copy-start
  7.2 0.8 reshape_squeeze.3
  8.0 0.8 fusion.4
  8.8 1.5 copy.66
  10.3 2.6 gather_fusion
  12.9 0.3 copy.67
  13.2 0.6 broadcast_multiply_fusion.4
  13.8 4.2 %all-to-all-start = ((f32[3,3,2,256]{3,1,0,2:T(4,128)}), f32[3,3,2,256]{3,1,0,2:T(4,128)S(1)}, u32[]{:S(2)}, u32[]{:S(2)}) async-start(f32[3,3,2,256]{3,1,0,2:T(4,128)} %broadcast_multiply_fusion.4), calls=%async_computation | async-start | bytes 49152 | tf_op jit(solution)/shard_map/all_to_all | solution.py:52
  18.9 3.1 %all-to-all-done = f32[3,3,2,256]{3,1,0,2:T(4,128)S(1)} async-done(((f32[3,3,2,256]{3,1,0,2:T(4,128)}), f32[3,3,2,256]{3,1,0,2:T(4,128)S(1)}, u32[]{:S(2)}, u32[]{:S(2)}) %all-to-all-start) | async-done | bytes 18464 | tf_op jit(solution)/shard_map/all_to_all | solution.py:52
  22.0 4.0 %collective-permute-start = (f32[3,1,2,256]{3,1,0,2:T(1,128)S(1)}, f32[3,1,2,256]{3,1,0,2:T(1,128)S(1)}, u32[]{:S(2)}, u32[]{:S(2)}) collective-permute-start(f32[3,1,2,256]{3,1,0,2:T(1,128)S(1)} %get-tuple-element.18), channel_id=1, source_target_pairs={{0,4},{4,8},{8,12},{1,5},{5,9},{9,13},{2,6},{6,10},{10,14},{3,7},{... | collective-permute-start | bytes 18440 | tf_op jit(solution)/shard_map/ppermute | solution.py:17
  25.9 1.3 collective-permute-start.1
  27.3 4.1 %collective-permute-done.1 = f32[3,1,2,256]{3,1,0,2:T(1,128)S(1)} collective-permute-done((f32[3,1,2,256]{3,1,0,2:T(1,128)S(1)}, f32[3,1,2,256]{3,1,0,2:T(1,128)S(1)}, u32[]{:S(2)}, u32[]{:S(2)}) %collective-permute-start.1) | collective-permute-done | bytes 6176 | tf_op jit(solution)/shard_map/ppermute | solution.py:19
  31.6 0.8 copy.71
  32.4 34.2 %gather_fusion.1 = f32[10240,3]{1,0:T(8,128)} fusion(f32[3,5632]{0,1:T(8,128)S(1)} %copy.71, s32[10240]{0:T(1024)S(1)} %broadcast_clamp_fusion), kind=kCustom, calls=%fused_computation.1 | custom fusion | bytes 286720 | tf_op jit(solution)/shard_map/gather | solution.py:64
  66.7 4.2 %copy.72 = f32[10,1024,3]{1,0,2:T(8,128)S(1)} copy(f32[10,1024,3]{2,1,0:T(8,128)} %bitcast.28) | data formatting | bytes 245760 | tf_op jit(solution)/shard_map/gather | solution.py:64
  70.9 0.3 broadcast_multiply_fusion.1
  71.2 0.1 reshape.145
  71.3 3.1 %copy.73 = f32[3,10240]{0,1:T(8,128)} copy(f32[3,10240]{1,0:T(4,128)S(1)} %reshape.145) | data formatting | bytes 245760 | tf_op jit(solution)/shard_map/reshape | solution.py:68
  74.4 51.9 %scatter_custom_fusion = f32[3,5632]{0,1:T(8,128)} fusion(s32[10240]{0:T(1024)S(1)} %bitcast.38, f32[3,10240]{0,1:T(8,128)} %copy.73, f32[]{:T(128)} %constant.7.clone.1), kind=kCustom, calls=%fused_computation.6 | custom fusion | flops 30720 | bytes 190468 | tf_op jit(solution)/shard_map/scatter-add | solution.py:70
  126.3 0.0 all-reduce.3.cloned.1.call-update
  126.3 22.3 %all-reduce.3.cloned.1.call-done = f32[3,5632]{0,1:T(8,128)} async-done(((f32[3,5632]{0,1:T(8,128)}), f32[3,5632]{0,1:T(8,128)}) %all-reduce.3.cloned.1.call-update) | async-done | bytes 67600 | tf_op jit(solution)/shard_map/psum | solution.py:72
  148.6 1.2 slice.55
  149.7 0.3 copy.74
  150.1 0.0 copy-start.4
  150.1 3.8 %collective-permute-start.2 = (f32[3,1,2,256]{3,1,0,2:T(1,128)S(1)}, f32[3,1,2,256]{3,1,0,2:T(1,128)S(1)}, u32[]{:S(2)}, u32[]{:S(2)}) collective-permute-start(f32[3,1,2,256]{3,1,0,2:T(1,128)S(1)} %get-tuple-element.16), channel_id=1, source_target_pairs={{0,4},{4,8},{8,12},{1,5},{5,9},{9,13},{2,6},{6,10},{10,14},{3,7},{... | collective-permute-start | bytes 18440 | tf_op jit(solution)/shard_map/ppermute | solution.py:17
  153.9 1.3 collective-permute-start.3
  155.2 0.0 collective-permute-done.2
  155.2 4.2 %collective-permute-done.3 = f32[3,1,2,256]{3,1,0,2:T(1,128)S(1)} collective-permute-done((f32[3,1,2,256]{3,1,0,2:T(1,128)S(1)}, f32[3,1,2,256]{3,1,0,2:T(1,128)S(1)}, u32[]{:S(2)}, u32[]{:S(2)}) %collective-permute-start.3) | collective-permute-done | bytes 6176 | tf_op jit(solution)/shard_map/ppermute | solution.py:19
  159.5 0.7 slice.40
  160.1 3.2 %all-to-all-start.1 = ((f32[3,3,2,256]{3,1,0,2:T(4,128)}), f32[3,3,2,256]{3,1,0,2:T(4,128)S(1)}, u32[]{:S(2)}, u32[]{:S(2)}) async-start(f32[3,3,2,256]{3,1,0,2:T(4,128)} %slice.40), calls=%async_computation.1 | async-start | bytes 49152 | tf_op jit(solution)/shard_map/all_to_all | solution.py:75
  163.4 3.9 %all-to-all-done.1 = f32[3,3,2,256]{3,1,0,2:T(4,128)S(1)} async-done(((f32[3,3,2,256]{3,1,0,2:T(4,128)}), f32[3,3,2,256]{3,1,0,2:T(4,128)S(1)}, u32[]{:S(2)}, u32[]{:S(2)}) %all-to-all-start.1) | async-done | bytes 18464 | tf_op jit(solution)/shard_map/all_to_all | solution.py:75
  167.3 0.3 copy.78
  167.6 9.5 %scatter_fusion = f32[3,4096]{0,1:T(8,128)S(1)} fusion(f32[3,4096]{0,1:T(8,128)S(1)} %slice-done, s32[1536]{0:T(1024)S(1)} %fusion.5, f32[1536,3]{1,0:T(8,128)S(1)} %copy.78), kind=kCustom, calls=%fused_computation.5 | custom fusion | flops 4608 | bytes 61440 | tf_op jit(solution)/shard_map/scatter-add | solution.py:79
  177.2 1.9 broadcast_multiply_fusion
  179.1 4.3 %gather_fusion.2 = f32[1536,3]{1,0:T(8,128)S(1)} fusion(f32[3,4096]{0,1:T(8,128)} %broadcast_multiply_fusion, s32[2048]{0:T(1024)S(1)} %pad_clamp_fusion), kind=kCustom, calls=%fused_computation.2 | custom fusion | bytes 43008 | tf_op jit(solution)/shard_map/gather | solution.py:51
  183.4 0.3 copy.79
  183.8 6.3 %all_to_all.15 = f32[3,3,2,256]{3,1,0,2:T(4,128)S(1)} all-to-all(f32[3,3,2,256]{3,1,0,2:T(4,128)S(1)} %broadcast_multiply_fusion.2), channel_id=1, replica_groups=mesh['groups'=2,'dom'=4,'sub'=2,'field'=2] {'sub'}, dimensions={2} | all-to-all | bytes 36864 | tf_op jit(solution)/shard_map/all_to_all | solution.py:52
  190.1 3.4 %collective-permute-start.4 = (f32[3,1,2,256]{3,1,0,2:T(1,128)S(1)}, f32[3,1,2,256]{3,1,0,2:T(1,128)S(1)}, u32[]{:S(2)}, u32[]{:S(2)}) collective-permute-start(f32[3,1,2,256]{3,1,0,2:T(1,128)S(1)} %get-tuple-element.14), channel_id=1, source_target_pairs={{0,4},{4,8},{8,12},{1,5},{5,9},{9,13},{2,6},{6,10},{10,14},{3,7},{... | collective-permute-start | bytes 18440 | tf_op jit(solution)/shard_map/ppermute | solution.py:17
  193.5 1.3 collective-permute-start.5
  194.8 0.0 collective-permute-done.4
  194.8 4.2 %collective-permute-done.5 = f32[3,1,2,256]{3,1,0,2:T(1,128)S(1)} collective-permute-done((f32[3,1,2,256]{3,1,0,2:T(1,128)S(1)}, f32[3,1,2,256]{3,1,0,2:T(1,128)S(1)}, u32[]{:S(2)}, u32[]{:S(2)}) %collective-permute-start.5) | collective-permute-done | bytes 6176 | tf_op jit(solution)/shard_map/ppermute | solution.py:19
  199.0 0.3 copy.83
  199.3 1.7 pad_maximum_fusion
  201.1 36.1 %gather_fusion.3 = f32[10240,3]{1,0:T(8,128)} fusion(f32[3,5632]{0,1:T(8,128)} %pad_maximum_fusion, s32[10240]{0:T(1024)S(1)} %broadcast_clamp_fusion), kind=kCustom, calls=%fused_computation.3 | custom fusion | bytes 286720 | tf_op jit(solution)/shard_map/gather | solution.py:82
  237.1 4.2 %copy.84 = f32[10,1024,3]{1,0,2:T(8,128)S(1)} copy(f32[10,1024,3]{2,1,0:T(8,128)} %bitcast.27) | data formatting | bytes 245760 | tf_op jit(solution)/shard_map/gather | solution.py:82
  241.4 0.6 multiply_reduce_fusion.1
  242.1 30.1 %all-reduce = (f32[]{:T(128)}, f32[]{:T(128)}, f32[]{:T(128)}, f32[]{:T(128)}) all-reduce(f32[]{:T(128)} %get-tuple-element.5, f32[]{:T(128)} %get-tuple-element.6, f32[]{:T(128)} %get-tuple-element.4, f32[]{:T(128)} %get-tuple-element.3), channel_id=1, replica_groups=mesh['groups'=2,'dom'=4,'sub'=2,'field'=2] {'dom','sub','field'}, use_global_device_ids=true, to_apply=%region_1.0 | all-reduce | flops 4 | bytes 32 | tf_op jit(solution)/shard_map/psum | solution.py:84
  276.2 0.6 multiply_add_fusion
  (53 shorter events, 0.5 us)
Async XLA Ops:
  7.2 63.7 %copy-start = (f32[30,30]{1,0:T(8,128)S(1)}, f32[30,30]{1,0:T(8,128)}, u32[]{:S(2)}) copy-start(f32[30,30]{1,0:T(8,128)} %param.23) | copy-start | bytes 10804
  7.2 24.4 %copy-start.2 = (f32[3,4096]{1,0:T(4,128)S(1)}, f32[3,4096]{1,0:T(4,128)}, u32[]{:S(2)}) copy-start(f32[3,4096]{1,0:T(4,128)} %param.12) | copy-start | bytes 147460
  7.2 10.9 %copy-start.3 = (s32[10,1024]{1,0:T(8,128)S(1)}, s32[10,1024]{1,0:T(8,128)}, u32[]{:S(2)}) copy-start(s32[10,1024]{1,0:T(8,128)} %param.14) | copy-start | bytes 122884
  7.2 20.0 %copy-start.7 = (f32[1024]{0:T(1024)S(1)}, f32[1024]{0:T(1024)}, u32[]{:S(2)}) copy-start(f32[1024]{0:T(1024)} %param.20) | copy-start | bytes 12292
  7.2 20.0 %copy-start.6 = (f32[1024]{0:T(1024)S(1)}, f32[1024]{0:T(1024)}, u32[]{:S(2)}) copy-start(f32[1024]{0:T(1024)} %param.16) | copy-start | bytes 12292
  13.8 8.1 %all-to-all-start = ((f32[3,3,2,256]{3,1,0,2:T(4,128)}), f32[3,3,2,256]{3,1,0,2:T(4,128)S(1)}, u32[]{:S(2)}, u32[]{:S(2)}) async-start(f32[3,3,2,256]{3,1,0,2:T(4,128)} %broadcast_multiply_fusion.4), calls=%async_computation | async-start | bytes 49152 | tf_op jit(solution)/shard_map/all_to_all | solution.py:52
  18.1 130.5 %all-reduce.3.cloned.1.call-start = ((), (), s32[]{:S(2)}) async-start(), calls=%async_computation.3 | async-start | bytes 5767168 | tf_op jit(solution)/shard_map/psum | solution.py:72
  22.0 5.3 %collective-permute-start = (f32[3,1,2,256]{3,1,0,2:T(1,128)S(1)}, f32[3,1,2,256]{3,1,0,2:T(1,128)S(1)}, u32[]{:S(2)}, u32[]{:S(2)}) collective-permute-start(f32[3,1,2,256]{3,1,0,2:T(1,128)S(1)} %get-tuple-element.18), channel_id=1, source_target_pairs={{0,4},{4,8},{8,12},{1,5},{5,9},{9,13},{2,6},{6,10},{10,14},{3,7},{... | collective-permute-start | bytes 18440 | tf_op jit(solution)/shard_map/ppermute | solution.py:17
  25.9 5.5 %collective-permute-start.1 = (f32[3,1,2,256]{3,1,0,2:T(1,128)S(1)}, f32[3,1,2,256]{3,1,0,2:T(1,128)S(1)}, u32[]{:S(2)}, u32[]{:S(2)}) collective-permute-start(f32[3,1,2,256]{3,1,0,2:T(1,128)S(1)} %get-tuple-element.19), channel_id=1, source_target_pairs={{4,0},{8,4},{12,8},{5,1},{9,5},{13,9},{6,2},{10,6},{14,10},{7,3},{... | collective-permute-start | bytes 18440 | tf_op jit(solution)/shard_map/ppermute | solution.py:19
  150.1 17.5 %slice-start = ((f32[3,5632]{0,1:T(8,128)}), f32[3,4096]{0,1:T(8,128)S(1)}, s32[]{:S(2)}) async-start(f32[3,5632]{0,1:T(8,128)} %all-reduce.3.cloned.1.call-done), calls=%async_computation.4 | async-start | bytes 4194304 | tf_op jit(solution)/shard_map/slice | solution.py:77
  150.1 27.0 %copy-start.4 = (f32[4096]{0:T(1024)S(1)}, f32[4096]{0:T(1024)}, u32[]{:S(2)}) copy-start(f32[4096]{0:T(1024)} %param.13) | copy-start | bytes 49156
  150.1 5.1 %collective-permute-start.2 = (f32[3,1,2,256]{3,1,0,2:T(1,128)S(1)}, f32[3,1,2,256]{3,1,0,2:T(1,128)S(1)}, u32[]{:S(2)}, u32[]{:S(2)}) collective-permute-start(f32[3,1,2,256]{3,1,0,2:T(1,128)S(1)} %get-tuple-element.16), channel_id=1, source_target_pairs={{0,4},{4,8},{8,12},{1,5},{5,9},{9,13},{2,6},{6,10},{10,14},{3,7},{... | collective-permute-start | bytes 18440 | tf_op jit(solution)/shard_map/ppermute | solution.py:17
  153.9 5.5 %collective-permute-start.3 = (f32[3,1,2,256]{3,1,0,2:T(1,128)S(1)}, f32[3,1,2,256]{3,1,0,2:T(1,128)S(1)}, u32[]{:S(2)}, u32[]{:S(2)}) collective-permute-start(f32[3,1,2,256]{3,1,0,2:T(1,128)S(1)} %get-tuple-element.17), channel_id=1, source_target_pairs={{4,0},{8,4},{12,8},{5,1},{9,5},{13,9},{6,2},{10,6},{14,10},{7,3},{... | collective-permute-start | bytes 18440 | tf_op jit(solution)/shard_map/ppermute | solution.py:19
  160.1 7.1 %all-to-all-start.1 = ((f32[3,3,2,256]{3,1,0,2:T(4,128)}), f32[3,3,2,256]{3,1,0,2:T(4,128)S(1)}, u32[]{:S(2)}, u32[]{:S(2)}) async-start(f32[3,3,2,256]{3,1,0,2:T(4,128)} %slice.40), calls=%async_computation.1 | async-start | bytes 49152 | tf_op jit(solution)/shard_map/all_to_all | solution.py:75
  179.1 20.2 %copy-start.1 = (f32[3,4096]{0,1:T(8,128)S(1)}, f32[3,4096]{0,1:T(8,128)}, u32[]{:S(2)}) copy-start(f32[3,4096]{0,1:T(8,128)} %broadcast_multiply_fusion) | copy-start | bytes 147460
  190.1 4.7 %collective-permute-start.4 = (f32[3,1,2,256]{3,1,0,2:T(1,128)S(1)}, f32[3,1,2,256]{3,1,0,2:T(1,128)S(1)}, u32[]{:S(2)}, u32[]{:S(2)}) collective-permute-start(f32[3,1,2,256]{3,1,0,2:T(1,128)S(1)} %get-tuple-element.14), channel_id=1, source_target_pairs={{0,4},{4,8},{8,12},{1,5},{5,9},{9,13},{2,6},{6,10},{10,14},{3,7},{... | collective-permute-start | bytes 18440 | tf_op jit(solution)/shard_map/ppermute | solution.py:17
  193.5 5.5 %collective-permute-start.5 = (f32[3,1,2,256]{3,1,0,2:T(1,128)S(1)}, f32[3,1,2,256]{3,1,0,2:T(1,128)S(1)}, u32[]{:S(2)}, u32[]{:S(2)}) collective-permute-start(f32[3,1,2,256]{3,1,0,2:T(1,128)S(1)} %get-tuple-element.15), channel_id=1, source_target_pairs={{4,0},{8,4},{12,8},{5,1},{9,5},{13,9},{6,2},{10,6},{14,10},{7,3},{... | collective-permute-start | bytes 18440 | tf_op jit(solution)/shard_map/ppermute | solution.py:19
  237.1 4.3 %copy-start.5 = (f32[1024]{0:T(1024)S(1)}, f32[1024]{0:T(1024)}, u32[]{:S(2)}) copy-start(f32[1024]{0:T(1024)} %param.19) | copy-start | bytes 12292
  237.1 4.3 %copy-start.8 = (f32[1024]{0:T(1024)S(1)}, f32[1024]{0:T(1024)}, u32[]{:S(2)}) copy-start(f32[1024]{0:T(1024)} %param.17) | copy-start | bytes 12292
  237.1 39.0 %copy-start.9 = (f32[1024]{0:T(1024)S(1)}, f32[1024]{0:T(1024)}, u32[]{:S(2)}) copy-start(f32[1024]{0:T(1024)} %param.18) | copy-start | bytes 12292
Sparse Core Ops, SparseCore 0:
  126.4 22.0 all-reduce.2
where the time goes:
time: 284 us
  local copies, waits for them, and re-layouts  95.7 us (34%)
  other arithmetic  67.9 us (24%)
  waiting for transfers between devices  41.8 us (15%)
  blocking collectives  36.4 us (13%)
  starting transfers between devices  22.5 us (8%)
  between operations  19.1 us (7%)
    scatter-add x1, other arithmetic, on_device(): jnp.zeros((3, owned_nodes + ghost_slots), jnp.float32).at[:, flat_connect]  51.9 us
    gather x2, local copies, waits for them, and re-layouts, on_device(): pulled = weighted_full[:, connect].reshape(30, element_count)  40.3 us
    gather x2, local copies, waits for them, and re-layouts, on_device(): element_state = state_full[:, connect].reshape(30, element_count)  38.4 us
    psum x1, blocking collectives, on_device(): lax.psum((jnp.sum(remain * remain), jnp.sum(search * hess_search), jnp.su...  30.1 us
    psum x1, waiting for transfers between devices, on_device(): accumulated = lax.psum(accumulated, 'field')  22.3 us
    ppermute x3, waiting for transfers between devices, extended(): lax.ppermute(head, axis, [((i + 1) % count, i) for i in range(ends)])  12.5 us
    ppermute x3, starting transfers between devices, extended(): lax.ppermute(tail, axis, [(i, (i + 1) % count) for i in range(ends)])  11.1 us
    scatter-add x1, other arithmetic, on_device(): assembled = accumulated[:, :owned_nodes] + jnp.zeros((3, owned_nodes), jn...  9.52 us
  transfers between devices with their start and end apart: 9, of which 6 were waited for; matrix products, arithmetic and copies ran while one was open for 0% of the time, Pallas kernels for 0%

commit v1 on v0

--- a/solution.py
+++ b/solution.py
@@ -4,6 +4,11 @@
 from jax.sharding import PartitionSpec as P
 
 BLK = 128
+
+
+def one_after_other(array, inner_axis, outer_axis):
+    half = lax.psum(array, inner_axis)
+    return lax.psum(half, outer_axis)
 
 
 def extended(cells, sides, width):
@@ -81,14 +86,15 @@
     weighted_full = fetch_ghosts(weighted)
     pulled = weighted_full[:, connect].reshape(30, element_count)
     hess_search = jnp.sum(coupled * pulled, axis=0) + reg_weight * search
-    squared_before, curvature_sum, cross_term, image_square = lax.psum(
+    squared_before, curvature_sum, cross_term, image_square = one_after_other(
         (
             jnp.sum(remain * remain),
             jnp.sum(search * hess_search),
             jnp.sum(remain * hess_search),
             jnp.sum(hess_search * hess_search),
         ),
-        ("dom", "sub", "field"),
+        ("sub", "field"),
+        "dom",
     )
     step_length = squared_before / curvature_sum
     iterate_next = guess + step_length * search

time: 284 us -> 271 us (0.954)
  blocking collectives: 36.4 us -> 23.2 us
    psum x1 -> x2, blocking collectives: 30.1 us -> 16.9 us  [the longest x1 10.5 us: one_after_other(): return lax.psum(half, outer_axis)]
where the time goes in v1:
time: 271 us
  local copies, waits for them, and re-layouts  95.7 us (35%)
  other arithmetic  68 us (25%)
  waiting for transfers between devices  41.8 us (15%)
  blocking collectives  23.2 us (9%)
  starting transfers between devices  22.5 us (8%)
  between operations  19.1 us (7%)
    scatter-add x1, other arithmetic, on_device(): jnp.zeros((3, owned_nodes + ghost_slots), jnp.float32).at[:, flat_connect]  51.9 us
    gather x2, local copies, waits for them, and re-layouts, on_device(): pulled = weighted_full[:, connect].reshape(30, element_count)  40.3 us
    gather x2, local copies, waits for them, and re-layouts, on_device(): element_state = state_full[:, connect].reshape(30, element_count)  38.5 us
    psum x1, waiting for transfers between devices, on_device(): accumulated = lax.psum(accumulated, 'field')  22.3 us
    ppermute x3, waiting for transfers between devices, extended(): lax.ppermute(head, axis, [((i + 1) % count, i) for i in range(ends)])  12.5 us
    ppermute x3, starting transfers between devices, extended(): lax.ppermute(tail, axis, [(i, (i + 1) % count) for i in range(ends)])  11.1 us
    psum x1, blocking collectives, one_after_other(): return lax.psum(half, outer_axis)  10.5 us
    scatter-add x1, other arithmetic, on_device(): assembled = accumulated[:, :owned_nodes] + jnp.zeros((3, owned_nodes), jn...  9.52 us
  transfers between devices with their start and end apart: 9, of which 6 were waited for; matrix products, arithmetic and copies ran while one was open for 0% of the time, Pallas kernels for 0%

profile of v1, /device:TPU:0, one launch (start us, length us, event | category | flops | bytes accessed | tf_op | source)
XLA Modules:
  0.0 270.5 jit_solution(7915630861587051021)
XLA Ops:
  7.2 0.0 copy-start
  7.2 0.8 reshape_squeeze.3
  8.0 0.8 fusion.4
  8.8 1.5 copy.66
  10.3 2.6 gather_fusion
  12.9 0.3 copy.67
  13.2 0.6 broadcast_multiply_fusion.4
  13.8 4.2 %all-to-all-start = ((f32[3,3,2,256]{3,1,0,2:T(4,128)}), f32[3,3,2,256]{3,1,0,2:T(4,128)S(1)}, u32[]{:S(2)}, u32[]{:S(2)}) async-start(f32[3,3,2,256]{3,1,0,2:T(4,128)} %broadcast_multiply_fusion.4), calls=%async_computation | async-start | bytes 49152 | tf_op jit(solution)/shard_map/all_to_all | solution.py:57
  18.9 3.1 %all-to-all-done = f32[3,3,2,256]{3,1,0,2:T(4,128)S(1)} async-done(((f32[3,3,2,256]{3,1,0,2:T(4,128)}), f32[3,3,2,256]{3,1,0,2:T(4,128)S(1)}, u32[]{:S(2)}, u32[]{:S(2)}) %all-to-all-start) | async-done | bytes 18464 | tf_op jit(solution)/shard_map/all_to_all | solution.py:57
  22.0 4.0 %collective-permute-start = (f32[3,1,2,256]{3,1,0,2:T(1,128)S(1)}, f32[3,1,2,256]{3,1,0,2:T(1,128)S(1)}, u32[]{:S(2)}, u32[]{:S(2)}) collective-permute-start(f32[3,1,2,256]{3,1,0,2:T(1,128)S(1)} %get-tuple-element.22), channel_id=1, source_target_pairs={{0,4},{4,8},{8,12},{1,5},{5,9},{9,13},{2,6},{6,10},{10,14},{3,7},{... | collective-permute-start | bytes 18440 | tf_op jit(solution)/shard_map/ppermute | solution.py:22
  25.9 1.3 collective-permute-start.1
  27.3 4.1 %collective-permute-done.1 = f32[3,1,2,256]{3,1,0,2:T(1,128)S(1)} collective-permute-done((f32[3,1,2,256]{3,1,0,2:T(1,128)S(1)}, f32[3,1,2,256]{3,1,0,2:T(1,128)S(1)}, u32[]{:S(2)}, u32[]{:S(2)}) %collective-permute-start.1) | collective-permute-done | bytes 6176 | tf_op jit(solution)/shard_map/ppermute | solution.py:24
  31.6 0.8 copy.71
  32.4 34.3 %gather_fusion.1 = f32[10240,3]{1,0:T(8,128)} fusion(f32[3,5632]{0,1:T(8,128)S(1)} %copy.71, s32[10240]{0:T(1024)S(1)} %broadcast_clamp_fusion), kind=kCustom, calls=%fused_computation.1 | custom fusion | bytes 286720 | tf_op jit(solution)/shard_map/gather | solution.py:69
  66.7 4.2 %copy.72 = f32[10,1024,3]{1,0,2:T(8,128)S(1)} copy(f32[10,1024,3]{2,1,0:T(8,128)} %bitcast.28) | data formatting | bytes 245760 | tf_op jit(solution)/shard_map/gather | solution.py:69
  70.9 0.3 broadcast_multiply_fusion.1
  71.2 0.1 reshape.145
  71.3 3.1 %copy.73 = f32[3,10240]{0,1:T(8,128)} copy(f32[3,10240]{1,0:T(4,128)S(1)} %reshape.145) | data formatting | bytes 245760 | tf_op jit(solution)/shard_map/reshape | solution.py:73
  74.4 51.9 %scatter_custom_fusion = f32[3,5632]{0,1:T(8,128)} fusion(s32[10240]{0:T(1024)S(1)} %bitcast.38, f32[3,10240]{0,1:T(8,128)} %copy.73, f32[]{:T(128)} %constant.7.clone.1), kind=kCustom, calls=%fused_computation.6 | custom fusion | flops 30720 | bytes 190468 | tf_op jit(solution)/shard_map/scatter-add | solution.py:75
  126.3 0.0 all-reduce.4.cloned.1.call-update
  126.3 22.3 %all-reduce.4.cloned.1.call-done = f32[3,5632]{0,1:T(8,128)} async-done(((f32[3,5632]{0,1:T(8,128)}), f32[3,5632]{0,1:T(8,128)}) %all-reduce.4.cloned.1.call-update) | async-done | bytes 67600 | tf_op jit(solution)/shard_map/psum | solution.py:77
  148.6 1.2 slice.55
  149.8 0.3 copy.74
  150.1 3.8 %collective-permute-start.2 = (f32[3,1,2,256]{3,1,0,2:T(1,128)S(1)}, f32[3,1,2,256]{3,1,0,2:T(1,128)S(1)}, u32[]{:S(2)}, u32[]{:S(2)}) collective-permute-start(f32[3,1,2,256]{3,1,0,2:T(1,128)S(1)} %get-tuple-element.20), channel_id=1, source_target_pairs={{0,4},{4,8},{8,12},{1,5},{5,9},{9,13},{2,6},{6,10},{10,14},{3,7},{... | collective-permute-start | bytes 18440 | tf_op jit(solution)/shard_map/ppermute | solution.py:22
  153.9 1.3 collective-permute-start.3
  155.2 0.0 collective-permute-done.2
  155.3 4.2 %collective-permute-done.3 = f32[3,1,2,256]{3,1,0,2:T(1,128)S(1)} collective-permute-done((f32[3,1,2,256]{3,1,0,2:T(1,128)S(1)}, f32[3,1,2,256]{3,1,0,2:T(1,128)S(1)}, u32[]{:S(2)}, u32[]{:S(2)}) %collective-permute-start.3) | collective-permute-done | bytes 6176 | tf_op jit(solution)/shard_map/ppermute | solution.py:24
  159.5 0.7 slice.40
  160.1 3.2 %all-to-all-start.1 = ((f32[3,3,2,256]{3,1,0,2:T(4,128)}), f32[3,3,2,256]{3,1,0,2:T(4,128)S(1)}, u32[]{:S(2)}, u32[]{:S(2)}) async-start(f32[3,3,2,256]{3,1,0,2:T(4,128)} %slice.40), calls=%async_computation.1 | async-start | bytes 49152 | tf_op jit(solution)/shard_map/all_to_all | solution.py:80
  163.4 3.9 %all-to-all-done.1 = f32[3,3,2,256]{3,1,0,2:T(4,128)S(1)} async-done(((f32[3,3,2,256]{3,1,0,2:T(4,128)}), f32[3,3,2,256]{3,1,0,2:T(4,128)S(1)}, u32[]{:S(2)}, u32[]{:S(2)}) %all-to-all-start.1) | async-done | bytes 18464 | tf_op jit(solution)/shard_map/all_to_all | solution.py:80
  167.3 0.3 copy.78
  167.6 9.5 %scatter_fusion = f32[3,4096]{0,1:T(8,128)S(1)} fusion(f32[3,4096]{0,1:T(8,128)S(1)} %slice-done, s32[1536]{0:T(1024)S(1)} %fusion.5, f32[1536,3]{1,0:T(8,128)S(1)} %copy.78), kind=kCustom, calls=%fused_computation.5 | custom fusion | flops 4608 | bytes 61440 | tf_op jit(solution)/shard_map/scatter-add | solution.py:84
  177.2 2.0 broadcast_multiply_fusion
  179.1 4.3 %gather_fusion.2 = f32[1536,3]{1,0:T(8,128)S(1)} fusion(f32[3,4096]{0,1:T(8,128)} %broadcast_multiply_fusion, s32[2048]{0:T(1024)S(1)} %pad_clamp_fusion), kind=kCustom, calls=%fused_computation.2 | custom fusion | bytes 43008 | tf_op jit(solution)/shard_map/gather | solution.py:56
  183.5 0.3 copy.79
  183.8 6.3 %all_to_all.15 = f32[3,3,2,256]{3,1,0,2:T(4,128)S(1)} all-to-all(f32[3,3,2,256]{3,1,0,2:T(4,128)S(1)} %broadcast_multiply_fusion.2), channel_id=1, replica_groups=mesh['groups'=2,'dom'=4,'sub'=2,'field'=2] {'sub'}, dimensions={2} | all-to-all | bytes 36864 | tf_op jit(solution)/shard_map/all_to_all | solution.py:57
  190.1 3.4 %collective-permute-start.4 = (f32[3,1,2,256]{3,1,0,2:T(1,128)S(1)}, f32[3,1,2,256]{3,1,0,2:T(1,128)S(1)}, u32[]{:S(2)}, u32[]{:S(2)}) collective-permute-start(f32[3,1,2,256]{3,1,0,2:T(1,128)S(1)} %get-tuple-element.18), channel_id=1, source_target_pairs={{0,4},{4,8},{8,12},{1,5},{5,9},{9,13},{2,6},{6,10},{10,14},{3,7},{... | collective-permute-start | bytes 18440 | tf_op jit(solution)/shard_map/ppermute | solution.py:22
  193.5 1.3 collective-permute-start.5
  194.8 0.0 collective-permute-done.4
  194.8 4.2 %collective-permute-done.5 = f32[3,1,2,256]{3,1,0,2:T(1,128)S(1)} collective-permute-done((f32[3,1,2,256]{3,1,0,2:T(1,128)S(1)}, f32[3,1,2,256]{3,1,0,2:T(1,128)S(1)}, u32[]{:S(2)}, u32[]{:S(2)}) %collective-permute-start.5) | collective-permute-done | bytes 6176 | tf_op jit(solution)/shard_map/ppermute | solution.py:24
  199.1 0.3 copy.83
  199.4 1.7 pad_maximum_fusion
  201.1 36.1 %gather_fusion.3 = f32[10240,3]{1,0:T(8,128)} fusion(f32[3,5632]{0,1:T(8,128)} %pad_maximum_fusion, s32[10240]{0:T(1024)S(1)} %broadcast_clamp_fusion), kind=kCustom, calls=%fused_computation.3 | custom fusion | bytes 286720 | tf_op jit(solution)/shard_map/gather | solution.py:87
  237.2 4.2 %copy.84 = f32[10,1024,3]{1,0,2:T(8,128)S(1)} copy(f32[10,1024,3]{2,1,0:T(8,128)} %bitcast.27) | data formatting | bytes 245760 | tf_op jit(solution)/shard_map/gather | solution.py:87
  241.5 0.7 multiply_reduce_fusion.1
  242.2 6.4 %all-reduce = (f32[]{:T(128)}, f32[]{:T(128)}, f32[]{:T(128)}, f32[]{:T(128)}) all-reduce(f32[]{:T(128)} %get-tuple-element.5, f32[]{:T(128)} %get-tuple-element.6, f32[]{:T(128)} %get-tuple-element.4, f32[]{:T(128)} %get-tuple-element.3), channel_id=1, replica_groups=mesh['groups'=2,'dom'=4,'sub'=2,'field'=2] {'sub','field'}, use_global_device_ids=true, to_apply=%region_1.0 | all-reduce | flops 4 | bytes 32 | tf_op jit(solution)/shard_map/psum | solution.py:10
  248.6 10.5 %all-reduce.1 = (f32[]{:T(128)}, f32[]{:T(128)}, f32[]{:T(128)}, f32[]{:T(128)}) all-reduce(f32[]{:T(128)} %get-tuple-element.7, f32[]{:T(128)} %get-tuple-element.8, f32[]{:T(128)} %get-tuple-element.9, f32[]{:T(128)} %get-tuple-element.10), channel_id=1, replica_groups=mesh['groups'=2,'dom'=4,'sub'=2,'field'=2] {'dom'}, use_global_device_ids=true, to_apply=%region_2.0 | all-reduce | flops 4 | bytes 32 | tf_op jit(solution)/shard_map/psum | solution.py:11
  263.1 0.6 multiply_add_fusion
  (54 shorter events, 0.5 us)
Async XLA Ops:
  7.2 63.8 %copy-start = (f32[30,30]{1,0:T(8,128)S(1)}, f32[30,30]{1,0:T(8,128)}, u32[]{:S(2)}) copy-start(f32[30,30]{1,0:T(8,128)} %param.23) | copy-start | bytes 10804
  7.2 24.4 %copy-start.2 = (f32[3,4096]{1,0:T(4,128)S(1)}, f32[3,4096]{1,0:T(4,128)}, u32[]{:S(2)}) copy-start(f32[3,4096]{1,0:T(4,128)} %param.12) | copy-start | bytes 147460
  7.2 10.9 %copy-start.3 = (s32[10,1024]{1,0:T(8,128)S(1)}, s32[10,1024]{1,0:T(8,128)}, u32[]{:S(2)}) copy-start(s32[10,1024]{1,0:T(8,128)} %param.14) | copy-start | bytes 122884
  7.2 20.0 %copy-start.7 = (f32[1024]{0:T(1024)S(1)}, f32[1024]{0:T(1024)}, u32[]{:S(2)}) copy-start(f32[1024]{0:T(1024)} %param.20) | copy-start | bytes 12292
  7.2 20.0 %copy-start.6 = (f32[1024]{0:T(1024)S(1)}, f32[1024]{0:T(1024)}, u32[]{:S(2)}) copy-start(f32[1024]{0:T(1024)} %param.16) | copy-start | bytes 12292
  13.8 8.1 %all-to-all-start = ((f32[3,3,2,256]{3,1,0,2:T(4,128)}), f32[3,3,2,256]{3,1,0,2:T(4,128)S(1)}, u32[]{:S(2)}, u32[]{:S(2)}) async-start(f32[3,3,2,256]{3,1,0,2:T(4,128)} %broadcast_multiply_fusion.4), calls=%async_computation | async-start | bytes 49152 | tf_op jit(solution)/shard_map/all_to_all | solution.py:57
  18.1 130.5 %all-reduce.4.cloned.1.call-start = ((), (), s32[]{:S(2)}) async-start(), calls=%async_computation.3 | async-start | bytes 5767168 | tf_op jit(solution)/shard_map/psum | solution.py:77
  22.0 5.3 %collective-permute-start = (f32[3,1,2,256]{3,1,0,2:T(1,128)S(1)}, f32[3,1,2,256]{3,1,0,2:T(1,128)S(1)}, u32[]{:S(2)}, u32[]{:S(2)}) collective-permute-start(f32[3,1,2,256]{3,1,0,2:T(1,128)S(1)} %get-tuple-element.22), channel_id=1, source_target_pairs={{0,4},{4,8},{8,12},{1,5},{5,9},{9,13},{2,6},{6,10},{10,14},{3,7},{... | collective-permute-start | bytes 18440 | tf_op jit(solution)/shard_map/ppermute | solution.py:22
  25.9 5.5 %collective-permute-start.1 = (f32[3,1,2,256]{3,1,0,2:T(1,128)S(1)}, f32[3,1,2,256]{3,1,0,2:T(1,128)S(1)}, u32[]{:S(2)}, u32[]{:S(2)}) collective-permute-start(f32[3,1,2,256]{3,1,0,2:T(1,128)S(1)} %get-tuple-element.23), channel_id=1, source_target_pairs={{4,0},{8,4},{12,8},{5,1},{9,5},{13,9},{6,2},{10,6},{14,10},{7,3},{... | collective-permute-start | bytes 18440 | tf_op jit(solution)/shard_map/ppermute | solution.py:24
  150.1 17.5 %slice-start = ((f32[3,5632]{0,1:T(8,128)}), f32[3,4096]{0,1:T(8,128)S(1)}, s32[]{:S(2)}) async-start(f32[3,5632]{0,1:T(8,128)} %all-reduce.4.cloned.1.call-done), calls=%async_computation.4 | async-start | bytes 4194304 | tf_op jit(solution)/shard_map/slice | solution.py:82
  150.1 27.1 %copy-start.4 = (f32[4096]{0:T(1024)S(1)}, f32[4096]{0:T(1024)}, u32[]{:S(2)}) copy-start(f32[4096]{0:T(1024)} %param.13) | copy-start | bytes 49156
  150.1 5.1 %collective-permute-start.2 = (f32[3,1,2,256]{3,1,0,2:T(1,128)S(1)}, f32[3,1,2,256]{3,1,0,2:T(1,128)S(1)}, u32[]{:S(2)}, u32[]{:S(2)}) collective-permute-start(f32[3,1,2,256]{3,1,0,2:T(1,128)S(1)} %get-tuple-element.20), channel_id=1, source_target_pairs={{0,4},{4,8},{8,12},{1,5},{5,9},{9,13},{2,6},{6,10},{10,14},{3,7},{... | collective-permute-start | bytes 18440 | tf_op jit(solution)/shard_map/ppermute | solution.py:22
  153.9 5.5 %collective-permute-start.3 = (f32[3,1,2,256]{3,1,0,2:T(1,128)S(1)}, f32[3,1,2,256]{3,1,0,2:T(1,128)S(1)}, u32[]{:S(2)}, u32[]{:S(2)}) collective-permute-start(f32[3,1,2,256]{3,1,0,2:T(1,128)S(1)} %get-tuple-element.21), channel_id=1, source_target_pairs={{4,0},{8,4},{12,8},{5,1},{9,5},{13,9},{6,2},{10,6},{14,10},{7,3},{... | collective-permute-start | bytes 18440 | tf_op jit(solution)/shard_map/ppermute | solution.py:24
  160.1 7.1 %all-to-all-start.1 = ((f32[3,3,2,256]{3,1,0,2:T(4,128)}), f32[3,3,2,256]{3,1,0,2:T(4,128)S(1)}, u32[]{:S(2)}, u32[]{:S(2)}) async-start(f32[3,3,2,256]{3,1,0,2:T(4,128)} %slice.40), calls=%async_computation.1 | async-start | bytes 49152 | tf_op jit(solution)/shard_map/all_to_all | solution.py:80
  179.1 20.2 %copy-start.1 = (f32[3,4096]{0,1:T(8,128)S(1)}, f32[3,4096]{0,1:T(8,128)}, u32[]{:S(2)}) copy-start(f32[3,4096]{0,1:T(8,128)} %broadcast_multiply_fusion) | copy-start | bytes 147460
  190.1 4.7 %collective-permute-start.4 = (f32[3,1,2,256]{3,1,0,2:T(1,128)S(1)}, f32[3,1,2,256]{3,1,0,2:T(1,128)S(1)}, u32[]{:S(2)}, u32[]{:S(2)}) collective-permute-start(f32[3,1,2,256]{3,1,0,2:T(1,128)S(1)} %get-tuple-element.18), channel_id=1, source_target_pairs={{0,4},{4,8},{8,12},{1,5},{5,9},{9,13},{2,6},{6,10},{10,14},{3,7},{... | collective-permute-start | bytes 18440 | tf_op jit(solution)/shard_map/ppermute | solution.py:22
  193.5 5.5 %collective-permute-start.5 = (f32[3,1,2,256]{3,1,0,2:T(1,128)S(1)}, f32[3,1,2,256]{3,1,0,2:T(1,128)S(1)}, u32[]{:S(2)}, u32[]{:S(2)}) collective-permute-start(f32[3,1,2,256]{3,1,0,2:T(1,128)S(1)} %get-tuple-element.19), channel_id=1, source_target_pairs={{4,0},{8,4},{12,8},{5,1},{9,5},{13,9},{6,2},{10,6},{14,10},{7,3},{... | collective-permute-start | bytes 18440 | tf_op jit(solution)/shard_map/ppermute | solution.py:24
  237.2 4.3 %copy-start.5 = (f32[1024]{0:T(1024)S(1)}, f32[1024]{0:T(1024)}, u32[]{:S(2)}) copy-start(f32[1024]{0:T(1024)} %param.19) | copy-start | bytes 12292
  237.2 4.3 %copy-start.8 = (f32[1024]{0:T(1024)S(1)}, f32[1024]{0:T(1024)}, u32[]{:S(2)}) copy-start(f32[1024]{0:T(1024)} %param.17) | copy-start | bytes 12292
  237.2 25.9 %copy-start.9 = (f32[1024]{0:T(1024)S(1)}, f32[1024]{0:T(1024)}, u32[]{:S(2)}) copy-start(f32[1024]{0:T(1024)} %param.18) | copy-start | bytes 12292
Sparse Core Ops, SparseCore 0:
  126.4 22.0 all-reduce.3
